TPU v7x, 256 devices: a whole 4x4x8 slice. The times are simulated.
256 devices in a mesh: cen: 32 (over y_lo, z, core), out: 8 (over x, y_hi).
Axes of the slice: x: 4, y: 4 (y_hi: 2, y_lo: 2; y = y_hi * 2 + y_lo), z: 8, core: 2. Of those that a mesh axis runs over, the one named last changes fastest.
Arguments:
- features: float32 [65536, 1024], P('cen', 'out'), may hold values from -6 to 6
- centres: float32 [65536, 1024], P('cen', 'out'), may hold values from -6 to 6
- coefs: float32 [65536, 1000], P('cen', 'out'), may hold values from -0.046875 to 0.046875
- batch_index: int32 [2, 512], P(None, 'cen'), may hold values from 0 to 2047
- targets: float32 [2, 512, 1000], P(None, 'cen', 'out'), may hold values from -6 to 6
Outputs:
- residuals: float32 [2, 512, 1000], P(None, 'cen', 'out')
- new_coefs: float32 [65536, 1000], P('cen', 'out')
All inputs are finite; a program needn't handle non-finite values.
Results may differ from a plain program's by a relative error of at most 0.0001.
Values sent between devices are 32-bit elements; how exact they have to be, the bound alone decides.
A program may use at most 64 MiB of HBM per device.

v0:
```python
import math

import jax
import jax.numpy as jnp
from jax import lax
from jax.sharding import Mesh
from jax.sharding import PartitionSpec as P

W = 1024
CEN = ("cen_0", "cen_1", "cen_2")
OUT = ("out_0", "out_1")
CEN_OUT = ("cen_0", "cen_1", "cen_2", "out_0", "out_1")


def sent_to_all(x, axis):
    size = lax.axis_size(axis)
    return lax.all_to_all(jnp.broadcast_to(x[None], (size, *x.shape)), axis, 0, 0, tiled=True)


def laid_out(parts, dim):
    parts = jnp.moveaxis(parts, 0, dim)
    shape = parts.shape
    return parts.reshape(*shape[:dim], shape[dim] * shape[dim + 1], *shape[dim + 2 :])


def gathered_copies(x, axis, dim):
    parts = sent_to_all(x, axis)
    return laid_out(parts, dim)


def cut_along(x, dim, size):
    shape = x.shape
    parts = x.reshape(*shape[:dim], size, shape[dim] // size, *shape[dim + 1 :])
    return jnp.moveaxis(parts, dim, 0)


def sum_at_owner(x, axis, dim):
    size = lax.axis_size(axis)
    parts = lax.all_to_all(cut_along(x, dim, size), axis, 0, 0, tiled=True)
    return jnp.sum(parts, axis=0)


def over_axes(x, axes):
    for axis in axes:
        x = lax.psum(x, axis)
    return x


def inner_rows(left, right):
    return lax.dot_general(
        left,
        right,
        (((1,), (1,)), ((), ())),
        precision=lax.Precision.HIGHEST,
        preferred_element_type=jnp.float32,
    )


def partial_squares(batch, centres, centre_sq):
    batch_sq = jnp.sum(batch * batch, axis=1)
    return batch_sq[:, None] + centre_sq[None, :] - 2.0 * inner_rows(batch, centres)


def laplace(squared):
    return jnp.exp(-jnp.sqrt(jnp.maximum(squared, 0.0)) / (0.5 * math.sqrt(W)))


def body(features, centres, coefs, batch_index, targets):
    local_rows = batch_index.shape[1]
    batch_total = local_rows * lax.axis_size(CEN)
    entries = centres.shape[0] * lax.axis_size(CEN) * coefs.shape[1] * lax.axis_size(OUT)
    full_centres = lax.all_gather(centres, OUT, axis=1, tiled=True)
    centre_sq = jnp.sum(full_centres * full_centres, axis=1)
    results = []
    grads = []
    sums = []
    for step in range(2):
        picked = jnp.take(features, batch_index[step], axis=0)
        batch = lax.all_gather(picked, CEN, axis=0, tiled=True)
        full_batch = gathered_copies(batch, OUT, 1)
        kern = laplace(partial_squares(full_batch, full_centres, centre_sq))
        predicted = sum_at_owner(
            jnp.dot(
                kern, coefs, precision=lax.Precision.HIGHEST, preferred_element_type=jnp.float32
            ),
            CEN,
            0,
        )
        resid = predicted - targets[step]
        results.append(resid)
        all_resid = gathered_copies(resid, CEN, 0)
        grad = (
            lax.dot_general(
                kern,
                all_resid,
                (((0,), (0,)), ((), ())),
                precision=lax.Precision.HIGHEST,
                preferred_element_type=jnp.float32,
            )
            / batch_total
        )
        grads.append(grad)
    sums = list(
        (
            over_axes(jnp.sum(grads[0] * grads[0]), CEN_OUT),
            over_axes(jnp.sum(grads[1] * grads[1]), CEN_OUT),
        )
    )
    new_coefs = coefs
    for step in range(2):
        scale = jnp.sqrt(sums[step] / entries + 1e-06)
        new_coefs = new_coefs - 0.1 * grads[step] / scale
    return (jnp.stack(results), new_coefs)


def solution(mesh):
    torus = Mesh(mesh.devices.reshape(2, 8, 2, 4, 2), ("cen_0", "cen_1", "cen_2", "out_0", "out_1"))
    return jax.shard_map(
        body,
        mesh=torus,
        in_specs=(P(CEN, OUT), P(CEN, OUT), P(CEN, OUT), P(None, CEN), P(None, CEN, OUT)),
        out_specs=(P(None, CEN, OUT), P(CEN, OUT)),
        check_vma=False,
    )
```

profile of v0, /device:TPU:1, one launch (start us, length us, event | category | flops | bytes accessed | tf_op | source)
XLA Modules:
  0.0 380.3 jit_solution(6459352137729763328)
XLA Ops:
  7.2 0.0 copy-start
  7.2 0.0 all-gather.2.cloned.1.call-start
  7.2 0.7 all-gather.2.cloned.1.call-update
  7.9 0.8 compare_and_fusion.1
  8.7 0.6 gather_fusion
  9.3 0.1 broadcast_select_fusion.1
  9.3 39.5 %all_gather.9 = f32[512,128]{1,0:T(8,128)S(1)} all-gather(f32[16,128]{1,0:T(8,128)S(1)} %broadcast_select_fusion.1), channel_id=1, replica_groups=mesh['cen_0'=2,'cen_1'=8,'cen_2'=2,'out_0'=4,'out_1'=2] {'cen_0','cen_1'..., dimensions={0}, use_global_device_ids=true | all-gather | bytes 270336 | tf_op jit(solution)/shard_map/all_gather | solution.py:79
  48.9 0.1 copy.7
  49.0 1.7 broadcast_in_dim.21
  50.7 6.4 %all-to-all-start = ((f32[8,512,128]{1,2,0:T(8,128)}), f32[8,512,128]{1,2,0:T(8,128)S(1)}, u32[]{:S(2)}, u32[]{:S(2)}) async-start(f32[8,512,128]{1,2,0:T(8,128)} %broadcast_in_dim.21), calls=%async_computation | async-start | bytes 4194304 | tf_op jit(solution)/shard_map/all_to_all | solution.py:17
  57.0 0.6 gather_fusion.1
  57.6 0.1 broadcast_select_fusion
  57.7 37.7 %all_gather.11 = f32[512,128]{1,0:T(8,128)} all-gather(f32[16,128]{1,0:T(8,128)S(1)} %broadcast_select_fusion), channel_id=1, replica_groups=mesh['cen_0'=2,'cen_1'=8,'cen_2'=2,'out_0'=4,'out_1'=2] {'cen_0','cen_1'..., dimensions={0}, use_global_device_ids=true | all-gather | bytes 270336 | tf_op jit(solution)/shard_map/all_gather | solution.py:79
  95.3 1.1 copy.8
  96.4 1.3 all-to-all-done
  97.7 1.8 broadcast_in_dim.22
  99.5 4.4 %all-to-all-start.2 = ((f32[8,512,128]{1,2,0:T(8,128)}), f32[8,512,128]{1,2,0:T(8,128)}, u32[]{:S(2)}, u32[]{:S(2)}) async-start(f32[8,512,128]{1,2,0:T(8,128)} %broadcast_in_dim.22), calls=%async_computation.2 | async-start | bytes 4194304 | tf_op jit(solution)/shard_map/all_to_all | solution.py:17
  103.8 0.2 fusion.1
  104.0 31.9 %all-to-all-done.2 = f32[8,512,128]{1,2,0:T(8,128)} async-done(((f32[8,512,128]{1,2,0:T(8,128)}), f32[8,512,128]{1,2,0:T(8,128)}, u32[]{:S(2)}, u32[]{:S(2)}) %all-to-all-start.2) | async-done | bytes 2097184 | tf_op jit(solution)/shard_map/all_to_all | solution.py:17
  135.9 1.8 fusion
  137.7 42.1 %all-gather.2.cloned.1.call-done = f32[2048,1024]{1,0:T(8,128)} async-done(((f32[2048,128]{1,0:T(8,128)}), f32[2048,1024]{1,0:T(8,128)}) %all-gather.2.cloned.1.call-update) | async-done | bytes 8388624 | tf_op jit(solution)/shard_map/all_gather | solution.py:72
  179.8 4.1 %multiply_reduce_fusion = f32[2048]{0:T(1024)S(1)} fusion(f32[2048,1024]{1,0:T(8,128)} %all-gather.2.cloned.1.call-done), kind=kLoop, calls=%fused_computation.2 | loop fusion | flops 4192256 | bytes 8396800 | tf_op jit(solution)/shard_map/reduce_sum | solution.py:73
  183.9 1.6 copy-done.4
  185.5 30.3 %multiply_exponential_fusion.1 = f32[512,2048]{1,0:T(8,128)S(1)} fusion(f32[512,1024]{0,1:T(8,128)} %bitcast.40, f32[2048,1024]{1,0:T(8,128)S(1)} %copy-done.4, f32[2048]{0:T(1024)S(1)} %multiply_reduce_fusion, f32[512]{0:T(512)S(1)} %fusion.1), kind=kOutput, calls=%fused_computation.4 | convolution fusion | flops 12891193344 | bytes 14690304 | tf_op jit(solution)/shard_map/dot_general | solution.py:50
  215.8 0.0 copy-start.1
  215.9 2.0 copy-done.1
  217.8 0.0 copy-done.3
  217.8 4.1 %fusion.2 = f32[512,125]{1,0:T(8,128)} fusion(f32[512,2048]{1,0:T(8,128)S(1)} %multiply_exponential_fusion.1, f32[2048,125]{1,0:T(8,128)S(1)} %copy-done.3), kind=kOutput, calls=%fused_computation.23 | convolution fusion | flops 1572864000 | bytes 5474304 | tf_op jit(solution)/shard_map/dot_general | solution.py:83
  222.0 5.1 %all-to-all-start.1 = ((f32[32,16,125]{2,1,0:T(8,128)}), f32[32,16,125]{2,1,0:T(8,128)S(1)}, u32[]{:S(2)}, u32[]{:S(2)}) async-start(f32[32,16,125]{2,1,0:T(8,128)} %bitcast.3), calls=%async_computation.1 | async-start | bytes 524288 | tf_op jit(solution)/shard_map/all_to_all | solution.py:39
  227.1 30.6 %multiply_exponential_fusion = f32[512,2048]{1,0:T(8,128)S(1)} fusion(f32[512,1024]{0,1:T(8,128)} %bitcast.7, f32[2048,1024]{1,0:T(8,128)} %all-gather.2.cloned.1.call-done, f32[512]{0:T(512)S(1)} %fusion, f32[2048]{0:T(1024)S(1)} %multiply_reduce_fusion), kind=kOutput, calls=%fused_computation.3 | convolution fusion | flops 12891193344 | bytes 14690304 | tf_op jit(solution)/shard_map/dot_general | solution.py:50
  257.7 1.9 copy-done.2
  259.6 4.1 %fusion.3 = f32[512,125]{1,0:T(8,128)} fusion(f32[512,2048]{1,0:T(8,128)S(1)} %multiply_exponential_fusion, f32[2048,125]{1,0:T(8,128)S(1)} %copy-done.3), kind=kOutput, calls=%fused_computation.24 | convolution fusion | flops 1572864000 | bytes 5474304 | tf_op jit(solution)/shard_map/dot_general | solution.py:83
  263.7 0.0 all-to-all-done.1
  263.7 8.4 %all-to-all-start.3 = ((f32[32,16,125]{2,1,0:T(8,128)}), f32[32,16,125]{2,1,0:T(8,128)S(1)}, u32[]{:S(2)}, u32[]{:S(2)}) async-start(f32[32,16,125]{2,1,0:T(8,128)} %bitcast.8), calls=%async_computation.3 | async-start | bytes 524288 | tf_op jit(solution)/shard_map/all_to_all | solution.py:39
  272.2 11.5 %all-to-all-done.3 = f32[32,16,125]{2,1,0:T(8,128)S(1)} async-done(((f32[32,16,125]{2,1,0:T(8,128)}), f32[32,16,125]{2,1,0:T(8,128)S(1)}, u32[]{:S(2)}, u32[]{:S(2)}) %all-to-all-start.3) | async-done | bytes 256032 | tf_op jit(solution)/shard_map/all_to_all | solution.py:39
  283.8 17.1 %all_to_all.30 = f32[32,16,125]{2,1,0:T(8,128)} all-to-all(f32[32,16,125]{2,1,0:T(8,128)S(1)} %broadcast_in_dim.46), channel_id=1, replica_groups=mesh['cen_0'=2,'cen_1'=8,'cen_2'=2,'out_0'=4,'out_1'=2] {'cen_0','cen_1'..., dimensions={0} | all-to-all | bytes 512000 | tf_op jit(solution)/shard_map/all_to_all | solution.py:17
  300.8 0.7 broadcast_in_dim.24
  301.5 5.1 %all-to-all-start.4 = ((f32[32,16,125]{2,1,0:T(8,128)}), f32[32,16,125]{2,1,0:T(8,128)S(1)}, u32[]{:S(2)}, u32[]{:S(2)}) async-start(f32[32,16,125]{2,1,0:T(8,128)} %broadcast_in_dim.24), calls=%async_computation.4 | async-start | bytes 524288 | tf_op jit(solution)/shard_map/all_to_all | solution.py:17
  306.7 0.6 pad_maximum_fusion
  307.3 9.1 %multiply_reduce_fusion.1 = (f32[]{:T(128)}, f32[2048,125]{1,0:T(8,128)S(1)}) fusion(f32[512,2048]{1,0:T(8,128)} %copy-done.2, f32[512,125]{1,0:T(8,128)} %bitcast.42), kind=kOutput, calls=%fused_computation.10 | convolution fusion | flops 1573632000 | bytes 5474308 | tf_op jit(solution)/shard_map/dot_general | solution.py:93
  316.4 2.2 all-to-all-done.4
  318.6 10.5 %multiply_reduce_fusion.2 = (f32[]{:T(128)}, f32[2048,125]{1,0:T(8,128)}) fusion(f32[512,2048]{1,0:T(8,128)} %copy-done.1, f32[512,125]{1,0:T(8,128)S(1)} %bitcast.41), kind=kOutput, calls=%fused_computation.11 | convolution fusion | flops 1573632000 | bytes 5474308 | tf_op jit(solution)/shard_map/dot_general | solution.py:93
  329.1 4.5 %all-reduce.4 = (f32[]{:T(128)}, f32[]{:T(128)}) all-reduce(f32[]{:T(128)} %get-tuple-element.21, f32[]{:T(128)} %get-tuple-element.23), channel_id=1, replica_groups=mesh['cen_0'=2,'cen_1'=8,'cen_2'=2,'out_0'=4,'out_1'=2] {'cen_0'}, use_global_device_ids=true, to_apply=%region_12.14 | all-reduce | flops 2 | bytes 16 | tf_op jit(solution)/shard_map/psum | solution.py:45
  333.6 11.9 %all-reduce = (f32[]{:T(128)}, f32[]{:T(128)}) all-reduce(f32[]{:T(128)} %get-tuple-element.11, f32[]{:T(128)} %get-tuple-element.12), channel_id=1, replica_groups=mesh['cen_0'=2,'cen_1'=8,'cen_2'=2,'out_0'=4,'out_1'=2] {'cen_1'}, use_global_device_ids=true, to_apply=%region_13.15 | all-reduce | flops 2 | bytes 16 | tf_op jit(solution)/shard_map/psum | solution.py:45
  345.5 9.2 %all-reduce.3 = (f32[]{:T(128)}, f32[]{:T(128)}) all-reduce(f32[]{:T(128)} %get-tuple-element.3, f32[]{:T(128)} %get-tuple-element.4), channel_id=1, replica_groups=mesh['cen_0'=2,'cen_1'=8,'cen_2'=2,'out_0'=4,'out_1'=2] {'cen_2'}, use_global_device_ids=true, to_apply=%region_14.16 | all-reduce | flops 2 | bytes 16 | tf_op jit(solution)/shard_map/psum | solution.py:45
  354.7 8.8 %all-reduce.1 = (f32[]{:T(128)}, f32[]{:T(128)}) all-reduce(f32[]{:T(128)} %get-tuple-element.9, f32[]{:T(128)} %get-tuple-element.10), channel_id=1, replica_groups=mesh['cen_0'=2,'cen_1'=8,'cen_2'=2,'out_0'=4,'out_1'=2] {'out_0'}, use_global_device_ids=true, to_apply=%region_15.17 | all-reduce | flops 2 | bytes 16 | tf_op jit(solution)/shard_map/psum | solution.py:45
  363.5 6.0 %all-reduce.2 = (f32[]{:T(128)}, f32[]{:T(128)}) all-reduce(f32[]{:T(128)} %get-tuple-element.5, f32[]{:T(128)} %get-tuple-element.6), channel_id=1, replica_groups=mesh['cen_0'=2,'cen_1'=8,'cen_2'=2,'out_0'=4,'out_1'=2] {'out_1'}, use_global_device_ids=true, to_apply=%region_16.18 | all-reduce | flops 2 | bytes 16 | tf_op jit(solution)/shard_map/psum | solution.py:45
  370.8 2.4 divide_subtract_fusion
  (14 shorter events, 0.1 us)
Async XLA Ops:
  7.2 1.5 copy-start
  7.2 172.6 %all-gather.2.cloned.1.call-start = ((), (), s32[]{:S(2)}) async-start(), calls=%async_computation.6 | async-start | bytes 9437184 | tf_op jit(solution)/shard_map/all_gather | solution.py:72
  50.7 47.0 %all-to-all-start = ((f32[8,512,128]{1,2,0:T(8,128)}), f32[8,512,128]{1,2,0:T(8,128)S(1)}, u32[]{:S(2)}, u32[]{:S(2)}) async-start(f32[8,512,128]{1,2,0:T(8,128)} %broadcast_in_dim.21), calls=%async_computation | async-start | bytes 4194304 | tf_op jit(solution)/shard_map/all_to_all | solution.py:17
  97.7 6.3 %copy-start.5 = (f32[8,512,128]{1,2,0:T(8,128)}, f32[8,512,128]{1,2,0:T(8,128)S(1)}, u32[]{:S(2)}) copy-start(f32[8,512,128]{1,2,0:T(8,128)S(1)} %all-to-all-done) | copy-start | bytes 6291460
  99.5 36.4 %all-to-all-start.2 = ((f32[8,512,128]{1,2,0:T(8,128)}), f32[8,512,128]{1,2,0:T(8,128)}, u32[]{:S(2)}, u32[]{:S(2)}) async-start(f32[8,512,128]{1,2,0:T(8,128)} %broadcast_in_dim.22), calls=%async_computation.2 | async-start | bytes 4194304 | tf_op jit(solution)/shard_map/all_to_all | solution.py:17
  179.8 5.8 %copy-start.4 = (f32[2048,1024]{1,0:T(8,128)S(1)}, f32[2048,1024]{1,0:T(8,128)}, u32[]{:S(2)}) copy-start(f32[2048,1024]{1,0:T(8,128)} %all-gather.2.cloned.1.call-done) | copy-start | bytes 25165828
  185.5 32.3 %copy-start.3 = (f32[2048,125]{1,0:T(8,128)S(1)}, f32[2048,125]{1,0:T(8,128)}, u32[]{:S(2)}) copy-start(f32[2048,125]{1,0:T(8,128)} %param.9) | copy-start | bytes 3072004
  215.8 2.0 copy-start.1
  222.0 41.7 %all-to-all-start.1 = ((f32[32,16,125]{2,1,0:T(8,128)}), f32[32,16,125]{2,1,0:T(8,128)S(1)}, u32[]{:S(2)}, u32[]{:S(2)}) async-start(f32[32,16,125]{2,1,0:T(8,128)} %bitcast.3), calls=%async_computation.1 | async-start | bytes 524288 | tf_op jit(solution)/shard_map/all_to_all | solution.py:39
  257.7 1.9 copy-start.2
  259.6 24.1 %copy-start.6 = (f32[2,16,125]{2,1,0:T(8,128)S(1)}, f32[2,16,125]{2,1,0:T(8,128)}, u32[]{:S(2)}) copy-start(f32[2,16,125]{2,1,0:T(8,128)} %param.11) | copy-start | bytes 48004
  263.7 20.0 %all-to-all-start.3 = ((f32[32,16,125]{2,1,0:T(8,128)}), f32[32,16,125]{2,1,0:T(8,128)S(1)}, u32[]{:S(2)}, u32[]{:S(2)}) async-start(f32[32,16,125]{2,1,0:T(8,128)} %bitcast.8), calls=%async_computation.3 | async-start | bytes 524288 | tf_op jit(solution)/shard_map/all_to_all | solution.py:39
  301.5 17.0 %all-to-all-start.4 = ((f32[32,16,125]{2,1,0:T(8,128)}), f32[32,16,125]{2,1,0:T(8,128)S(1)}, u32[]{:S(2)}, u32[]{:S(2)}) async-start(f32[32,16,125]{2,1,0:T(8,128)} %broadcast_in_dim.24), calls=%async_computation.4 | async-start | bytes 524288 | tf_op jit(solution)/shard_map/all_to_all | solution.py:17
Sparse Core Ops, SparseCore 0:
  10.5 169.2 all-gather.1
where the time goes:
time: 385 us; the launch traced here: 380 us
  blocking collectives  135 us (35%)
  waiting for transfers between devices  89.6 us (23%)
  matrix products  88.7 us (23%)
  starting transfers between devices  29.4 us (8%)
  between operations  15.7 us (4%)
  local copies, waits for them, and re-layouts  12 us (3%)
  other arithmetic  10.2 us (3%)
    all_gather x2, blocking collectives, body(): batch = lax.all_gather(picked, CEN, axis=0, tiled=True)  77.2 us
    dot_general x2, matrix products, inner_rows(): lax.dot_general(left, right, (((1,), (1,)), ((), ())), precision=lax.Prec...  60.9 us
    all_gather x1, waiting for transfers between devices, body(): full_centres = lax.all_gather(centres, OUT, axis=1, tiled=True)  42.1 us
    psum x5, blocking collectives, over_axes(): x = lax.psum(x, axis)  40.4 us
    all_to_all x3, waiting for transfers between devices, sent_to_all(): lax.all_to_all(jnp.broadcast_to(x[None], (size, *x.shape)), axis, 0, 0, t...  35.3 us
    dot_general x2, matrix products, body(): lax.dot_general(kern, all_resid, (((0,), (0,)), ((), ())), precision=lax....  19.6 us
    all_to_all x1, blocking collectives, sent_to_all(): lax.all_to_all(jnp.broadcast_to(x[None], (size, *x.shape)), axis, 0, 0, t...  17.1 us
    all_to_all x3, starting transfers between devices, sent_to_all(): lax.all_to_all(jnp.broadcast_to(x[None], (size, *x.shape)), axis, 0, 0, t...  15.8 us
  transfers between devices with their start and end apart: 6, of which 5 were waited for; matrix products, arithmetic and copies ran while one was open for 14% of the time, Pallas kernels for 0%

commit v1 on v0

v1 whole, which is shorter than its diff:
```python
import functools
import math

import jax
import jax.numpy as jnp
from jax import lax
from jax.experimental import pallas as pl
from jax.experimental.pallas import tpu as pltpu
from jax.sharding import Mesh
from jax.sharding import PartitionSpec as P

W = 1024
LANES = 128
CEN = ("cen_0", "cen_1", "cen_2")
OUT = ("out_0", "out_1")
MESH = pl.DeviceIdType.MESH
NX, NY, NZ = 4, 4, 8
F32, BF16 = jnp.float32, jnp.bfloat16


def halves(v):
    hi = v.astype(BF16)
    return hi, (v - hi.astype(F32)).astype(BF16)


def dot_rows(a, b):
    return lax.dot_general(a, b, (((1,), (1,)), ((), ())), preferred_element_type=F32)


def dot_plain(a, b):
    return lax.dot_general(a, b, (((1,), (0,)), ((), ())), preferred_element_type=F32)


def kernel(
    entries, idx_ref, feat_ref, cen_ref, coef_ref, targ_ref, upd_ref, res_ref,
    cpad, bs, cs, gs, chi, clo, ghi, glo, sbh, sbl, kf, kth, ktl,
    psend, precv, q, rx0, s0, ry0, ry1, t1, rx1, tz, rz, rb, rhi, rlo,
    g, us, pv, pd, pz, pp,
    pl_s, pl_r, cx_s, cx_r, cy_s, cy_r, gx_s, gx_r, z_s, z_r, d_s, d_r,
    pr_s, pr_r, x0_s, x0_r, y0_s, y0_r, y1_s, y1_r, x1_s, x1_r, rz_s, rz_r,
    az_s, az_r, ay0_s, ay0_r, ax0_s, ax0_r, ax1_s, ax1_r, ay1_s, ay1_r, ad_s, ad_r,
    p_s, p_r, u_s, u_r,
):
    x, yh = lax.axis_index("out_0"), lax.axis_index("out_1")
    yl, z, c = lax.axis_index("cen_0"), lax.axis_index("cen_1"), lax.axis_index("cen_2")
    y = yh * 2 + yl
    rows = cen_ref.shape[0] // NX
    blk = yh * NX + x

    def at_x(d):
        return lax.rem(x + d, NX)

    def at_z(d):
        return lax.rem(z + d + NZ, NZ)

    def to(dx=0, dy=0, dz=0, flip=False):
        ny = lax.rem(y + dy, NY)
        return {
            "out_0": at_x(dx), "out_1": lax.div(ny, 2), "cen_0": lax.rem(ny, 2),
            "cen_1": at_z(dz), "cen_2": 1 - c if flip else c,
        }

    pair_y = {"out_0": x, "out_1": yh, "cen_0": 1 - yl, "cen_1": z, "cen_2": c}
    plane = [(dx, dy) for dx in range(NX) for dy in range(NY) if dx or dy]
    peers = [to(dx, dy) for dx, dy in plane] + [to(dz=d) for d in range(1, NZ)] + [to(flip=True)]

    barrier = pltpu.get_barrier_semaphore()
    for peer in peers:
        pl.semaphore_signal(barrier, inc=1, device_id=peer, device_id_type=MESH)

    sent = []

    def send(src, dst, ss, rs, dev):
        copy = pltpu.make_async_remote_copy(
            src_ref=src, dst_ref=dst, send_sem=ss, recv_sem=rs, device_id=dev, device_id_type=MESH
        )
        copy.start()
        sent.append(copy)
        return copy

    mine = bs.at[z, c, yl, blk]
    for k in range(2):
        for j in range(16):
            mine[pl.ds(k * 16 + j, 1), :] = feat_ref[pl.ds(idx_ref[k, j], 1), :]
    cs[blk] = cen_ref[pl.ds(pl.multiple_of(x * rows, 8), rows), :]
    wide = coef_ref.shape[1]

    @pl.loop(0, cpad.shape[0] // 256)
    def _(i):
        at = pl.ds(pl.multiple_of(i * 256, 256), 256)
        cpad[at, :] = jnp.zeros((256, LANES), F32)
        cpad[at, pl.ds(0, wide)] = coef_ref[at, :]

    gs[x] = cpad[pl.ds(pl.multiple_of(x * rows, 8), rows), :]
    pl.semaphore_wait(barrier, len(peers))

    got_plane = [
        send(mine, mine, pl_s.at[n], pl_r.at[n], to(dx, dy)) for n, (dx, dy) in enumerate(plane)
    ]
    got_cx = {}
    for d in (2, 1, 3):
        src = cen_ref.at[pl.ds(pl.multiple_of(at_x(d) * rows, 8), rows)]
        got_cx[d] = send(src, cs.at[blk], cx_s.at[d - 1], cx_r.at[d - 1], to(dx=d))
    own = cen_ref.at[pl.ds(pl.multiple_of(x * rows, 8), rows)]
    got_cy = {0: send(own, cs.at[blk], cy_s.at[0], cy_r.at[0], to(dy=2))}

    for copy in got_plane:
        copy.wait_recv()
    got_z, got_d = {}, {}
    for h in range(2):
        part = bs.at[z, c, h]
        for way, dz in ((0, 1), (1, -1)):
            got_z[way, 1, h] = send(part, part, z_s.at[way, 0, h], z_r.at[way, 0, h], to(dz=dz))
    for h in range(2):
        part = bs.at[z, c, h]
        got_d[0, h] = send(part, part, d_s.at[0, h], d_r.at[0, h], to(flip=True))

    for d in (1, 3, 2):
        got_cx[d].wait_recv()
        part = cs.at[yh * NX + at_x(NX - d)]
        got_cy[d] = send(part, part, cy_s.at[d], cy_r.at[d], to(dy=2))
    got_g = []
    for d in range(1, NX):
        src = cpad.at[pl.ds(pl.multiple_of(at_x(d) * rows, 8), rows)]
        got_g.append(send(src, gs.at[x], gx_s.at[d - 1], gx_r.at[d - 1], to(dx=d)))

    def ring_step(s):
        for h in range(2):
            for way, dz in ((0, 1), (1, -1)):
                if s == 4 and h != way:
                    continue
                got_z[way, s, h].wait_recv()
                part = bs.at[at_z(-dz * s), c, h]
                if s < 3 or (s == 3 and h == way):
                    got_z[way, s + 1, h] = send(
                        part, part, z_s.at[way, s, h], z_r.at[way, s, h], to(dz=dz)
                    )
                rel = (-dz * s) % NZ
                got_d[rel, h] = send(part, part, d_s.at[rel, h], d_r.at[rel, h], to(flip=True))

    def take_centres(base):
        for i in range(NX):
            v = cs[base + i]
            hi, lo = halves(v)
            at = pl.ds(pl.multiple_of((base + i) * LANES, LANES), LANES)
            chi[:, at] = hi
            clo[:, at] = lo

    take_centres(yh * NX)
    ring_step(1)
    ring_step(2)
    ring_step(3)
    for d in range(NX):
        got_cy[d].wait_recv()
    take_centres((1 - yh) * NX)
    total = cs[0] * cs[0]
    for i in range(1, 2 * NX):
        total = total + cs[i] * cs[i]
    centre_sq = jnp.sum(total.T, axis=0, keepdims=True)

    def kernel_slab(rel):
        zs = at_z(rel)
        for h in range(2):
            got_d[rel, h].wait_recv()
        squares = []
        for cc in range(2):
            for h in range(2):
                at = pl.ds((cc * 2 + h) * 32, 32)
                acc = None
                for b in range(2 * NX):
                    v = bs[zs, cc, h, b]
                    hi, lo = halves(v)
                    sbh[at, pl.ds(b * LANES, LANES)] = hi
                    sbl[at, pl.ds(b * LANES, LANES)] = lo
                    acc = v * v if acc is None else acc + v * v
                squares.append(jnp.sum(acc, axis=1, keepdims=True))
        batch_sq = jnp.concatenate(squares, axis=0)
        bh, bl = sbh[...], sbl[...]
        for n in range(rows // 256):
            cat = pl.ds(n * 256, 256)
            ch, cl = chi[cat, :], clo[cat, :]
            inner = (dot_rows(bl, cl) + dot_rows(bl, ch)) + dot_rows(bh, cl) + dot_rows(bh, ch)
            sq = batch_sq + centre_sq[:, n * 256 : (n + 1) * 256] - 2.0 * inner
            kern = jnp.exp(jnp.sqrt(jnp.maximum(sq, 0.0)) * (-1.0 / (0.5 * math.sqrt(W))))
            for cc in range(2):
                for h in range(2):
                    for k in range(2):
                        r = (cc * 2 + h) * 32 + k * 16
                        kf[k, cc, h, pl.ds(pl.multiple_of(zs * 16, 16), 16), cat] = kern[r : r + 16]

    for rel in (0, 1, 7, 2, 6, 3, 5):
        kernel_slab(rel)
    for copy in got_g:
        copy.wait_recv()
    for i in range(NX):
        hi, lo = halves(gs[i])
        ghi[:, pl.ds(i * LANES, LANES)] = hi
        glo[:, pl.ds(i * LANES, LANES)] = lo
    ring_step(4)
    kernel_slab(4)

    def predict(k, cc, h):
        kh, kl = halves(kf[k, cc, h])
        return dot_plain(kl, ghi[...]) + dot_plain(kh, glo[...]) + dot_plain(kh, ghi[...])

    got_p = {}
    for k in (1, 0):
        for h in range(2):
            out = predict(k, 1 - c, h)
            for i in range(NX):
                psend[k, i, h] = out[:, i * LANES : (i + 1) * LANES]
        got_p[k] = send(psend.at[k], precv.at[k], pr_s.at[k], pr_r.at[k], to(flip=True))
    for k in (1, 0):
        for h in range(2):
            out = predict(k, c, h)
            for i in range(NX):
                q[k, i, h] = out[:, i * LANES : (i + 1) * LANES]

    def join(k):
        got_p[k].wait_recv()
        for i in range(NX):
            for h in range(2):
                q[k, i, h] = q[k, i, h] + precv[k, i, h]

    join(1)
    got_y1 = send(q.at[1, :, 1 - yl], ry1, y1_s.at[0], y1_r.at[0], pair_y)
    join(0)
    got_x0 = [
        send(q.at[0, at_x(d)], rx0.at[d - 1], x0_s.at[d - 1], x0_r.at[d - 1], to(dx=d))
        for d in (2, 1, 3)
    ]
    for k in range(2):
        for cc in range(2):
            for h in range(2):
                for n in range(rows // 128):
                    hi, lo = halves(kf[k, cc, h, :, pl.ds(n * 128, 128)].T)
                    at = pl.ds((cc * 2 + h) * 128, 128)
                    kth[k, pl.ds(n * 128, 128), at] = hi
                    ktl[k, pl.ds(n * 128, 128), at] = lo
    got_y1.wait_recv()
    for i in range(NX):
        t1[i] = q[1, i, yl] + ry1[i]
    got_x1 = [
        send(t1.at[at_x(d)], rx1.at[d - 1], x1_s.at[d - 1], x1_r.at[d - 1], to(dx=d))
        for d in (2, 1, 3)
    ]
    for copy in got_x0:
        copy.wait_recv()
    for h in range(2):
        s0[h] = (q[0, x, h] + rx0[0, h]) + (rx0[1, h] + rx0[2, h])
    got_y0 = send(s0.at[1 - yl], ry0, y0_s.at[0], y0_r.at[0], pair_y)

    def spread_z(k):
        return [
            send(tz.at[k, at_z(d)], rz.at[k, d - 1], rz_s.at[k, d - 1], rz_r.at[k, d - 1], to(dz=d))
            for d in range(1, NZ)
        ]

    for copy in got_x1:
        copy.wait_recv()
    tz[1] = ((t1[x] + rx1[0]) + (rx1[1] + rx1[2])).reshape(NZ, 16, LANES)
    got_z1 = spread_z(1)
    got_y0.wait_recv()
    tz[0] = (s0[yl] + ry0[...]).reshape(NZ, 16, LANES)
    got_z0 = spread_z(0)

    def residual(k, got):
        for copy in got:
            copy.wait_recv()
        acc = tz[k, z]
        for d in range(1, NZ):
            acc = acc + rz[k, d - 1]
        at = pl.ds(pl.multiple_of(z * 16, 16), 16)
        rb[k, x, c, yl, at, :] = jnp.zeros((16, LANES), F32)
        rb[k, x, c, yl, at, pl.ds(0, wide)] = acc[:, :wide] - targ_ref[k]
        block = rb.at[k, x, c, yl, at]
        res_ref[k] = block[...]
        return [
            send(block, block, az_s.at[k, d - 1], az_r.at[k, d - 1], to(dz=d)) for d in range(1, NZ)
        ]

    got_a1 = residual(1, got_z1)
    got_a0 = residual(0, got_z0)

    for copy in got_a1:
        copy.wait_recv()
    part = rb.at[1, x, c, yl]
    got_ax1 = [send(part, part, ax1_s.at[d - 1], ax1_r.at[d - 1], to(dx=d)) for d in (2, 1, 3)]
    for copy in got_a0:
        copy.wait_recv()
    part = rb.at[0, x, c, yl]
    got_ay0 = send(part, part, ay0_s.at[0], ay0_r.at[0], pair_y)
    for copy in got_ax1:
        copy.wait_recv()
    part = rb.at[1, :, c, yl]
    got_ay1 = send(part, part, ay1_s.at[0], ay1_r.at[0], pair_y)
    got_ad = {1: [], 0: []}
    got_ad[1].append(send(part, part, ad_s.at[0], ad_r.at[0], to(flip=True)))
    got_ay0.wait_recv()
    part = rb.at[0, x, c]
    got_ax0 = {
        d: send(part, part, ax0_s.at[d - 1], ax0_r.at[d - 1], to(dx=d)) for d in (2, 1, 3)
    }
    got_ad[0].append(send(part, part, ad_s.at[1], ad_r.at[1], to(flip=True)))
    for d in (1, 3, 2):
        got_ax0[d].wait_recv()
        part = rb.at[0, at_x(NX - d), c]
        got_ad[0].append(send(part, part, ad_s.at[1 + d], ad_r.at[1 + d], to(flip=True)))
    got_ay1.wait_recv()
    part = rb.at[1, :, c, 1 - yl]
    got_ad[1].append(send(part, part, ad_s.at[5], ad_r.at[5], to(flip=True)))

    def gradient(k):
        for copy in got_ad[k]:
            copy.wait_recv()
        for i in range(NX):
            for cc in range(2):
                for h in range(2):
                    hi, lo = halves(rb[k, i, cc, h])
                    at = pl.ds((cc * 2 + h) * 128, 128)
                    rhi[at, pl.ds(i * LANES, LANES)] = hi
                    rlo[at, pl.ds(i * LANES, LANES)] = lo
        acc = jnp.zeros((8, LANES), F32)
        for n in range(rows // 128):
            at = pl.ds(n * 128, 128)
            kh, kl = kth[k, at, :], ktl[k, at, :]
            out = dot_plain(kl, rhi[...]) + dot_plain(kh, rlo[...]) + dot_plain(kh, rhi[...])
            out = out * (1.0 / (2 * NZ * 2 * 16))
            for i in range(NX):
                v = out[:, i * LANES : (i + 1) * LANES]
                g[k, i, at, :] = v
                acc = acc + jnp.sum((v * v).reshape(16, 8, LANES), axis=0)
        pv[k] = acc

    gradient(0)
    gradient(1)

    got = send(pv, pd, p_s.at[0], p_r.at[0], to(flip=True))
    got.wait_recv()
    pz[...] = pv[...] + pd[...]
    acc = pz[...]
    got = [
        send(pz, pp.at[d], p_s.at[d], p_r.at[d], to(dz=d)) for d in range(1, NZ)
    ]
    for d, copy in enumerate(got, 1):
        copy.wait_recv()
        acc = acc + pp[d]
    pp[0] = acc
    got = [
        send(pp.at[0], pp.at[8 + n], p_s.at[8 + n], p_r.at[8 + n], to(dx, dy))
        for n, (dx, dy) in enumerate(plane)
    ]
    for n, copy in enumerate(got):
        copy.wait_recv()
        acc = acc + pp[8 + n]
    factor = []
    for k in range(2):
        sums = jnp.sum(jnp.sum(acc[k], axis=0, keepdims=True), axis=1, keepdims=True)
        factor.append(0.1 / jnp.sqrt(sums / entries + 1e-6))

    got = []
    for d in (2, 1, 3):
        us[d - 1] = g[0, at_x(d)] * factor[0] + g[1, at_x(d)] * factor[1]
        here = upd_ref.at[pl.ds(pl.multiple_of(x * rows, 8), rows)]
        got.append(send(us.at[d - 1], here, u_s.at[d - 1], u_r.at[d - 1], to(dx=d)))
    upd_ref[pl.ds(pl.multiple_of(x * rows, 8), rows), :] = g[0, x] * factor[0] + g[1, x] * factor[1]
    for copy in got:
        copy.wait_recv()
    for copy in sent:
        copy.wait_send()


def body(features, centres, coefs, batch_index, targets):
    total = centres.shape[0]
    rows = total // NX
    entries = total * lax.axis_size(CEN) * coefs.shape[1] * lax.axis_size(OUT)
    vm = lambda *shape: pltpu.VMEM(shape, F32)
    vb = lambda *shape: pltpu.VMEM(shape, BF16)
    dma = lambda *shape: pltpu.SemaphoreType.DMA(shape)
    two = lambda *shape: [dma(*shape), dma(*shape)]
    scratch = [
        vm(total, LANES), vm(8, 2, 2, 8, 32, LANES), vm(8, rows, LANES), vm(NX, rows, LANES),
        vb(rows, W), vb(rows, W), vb(rows, 512), vb(rows, 512), vb(128, W), vb(128, W),
        vm(2, 2, 2, 128, rows), vb(2, rows, 512), vb(2, rows, 512),
        vm(2, NX, 2, 128, LANES), vm(2, NX, 2, 128, LANES), vm(2, NX, 2, 128, LANES),
        vm(3, 2, 128, LANES), vm(2, 128, LANES), vm(128, LANES), vm(NX, 128, LANES),
        vm(NX, 128, LANES), vm(3, 128, LANES), vm(2, NZ, 16, LANES), vm(2, 7, 16, LANES),
        vm(2, NX, 2, 2, 128, LANES), vb(512, 512), vb(512, 512),
        vm(2, NX, rows, LANES), vm(3, rows, LANES),
        vm(2, 8, LANES), vm(2, 8, LANES), vm(2, 8, LANES), vm(23, 2, 8, LANES),
        *two(15), *two(3), *two(4), *two(3), *two(2, 4, 2), *two(8, 2),
        *two(2), *two(3), *two(1), *two(1), *two(3), *two(2, 7),
        *two(2, 7), *two(1), *two(3), *two(3), *two(1), *two(6),
        *two(23), *two(3),
    ]
    whole = pl.BlockSpec(memory_space=pltpu.VMEM)
    upd, resid = pl.pallas_call(
        functools.partial(kernel, float(entries)),
        out_shape=(
            jax.ShapeDtypeStruct((total, LANES), F32),
            jax.ShapeDtypeStruct((2, 16, LANES), F32),
        ),
        in_specs=[pl.BlockSpec(memory_space=pltpu.SMEM)] + [whole] * 4,
        out_specs=(whole, whole),
        scratch_shapes=scratch,
        compiler_params=pltpu.CompilerParams(
            collective_id=0, has_side_effects=True, vmem_limit_bytes=60 * 2**20
        ),
        name="step",
    )(batch_index, features, centres, coefs, targets)
    wide = coefs.shape[1]
    return resid[:, :, :wide], coefs - upd[:, :wide]


def solution(mesh):
    torus = Mesh(mesh.devices.reshape(2, 8, 2, 4, 2), ("cen_0", "cen_1", "cen_2", "out_0", "out_1"))
    return jax.shard_map(
        body,
        mesh=torus,
        in_specs=(P(CEN, OUT), P(CEN, OUT), P(CEN, OUT), P(None, CEN), P(None, CEN, OUT)),
        out_specs=(P(None, CEN, OUT), P(CEN, OUT)),
        check_vma=False,
    )
```

time: 385 us -> 132 us (0.34); the launches traced: 380 us -> 132 us
  blocking collectives: 135 us -> 0 us
  Pallas kernels: 0 us -> 128 us
  waiting for transfers between devices: 89.6 us -> 0 us
  matrix products: 88.7 us -> 0 us
  starting transfers between devices: 29.4 us -> 0 us
  between operations: 15.7 us -> 0.66 us
  local copies, waits for them, and re-layouts: 12 us -> 0.61 us
  other arithmetic: 10.2 us -> 2.31 us
    pallas_call x0 -> x1, Pallas kernels: none -> 128 us  [body(): pl.pallas_call(functools.partial(kernel, float(entries)), out_shape=(jax....]
    dot_general x6 -> x0, matrix products: 88.7 us -> none  [the longest x2 60.9 us: inner_rows(): lax.dot_general(left, right, (((1,), (1,)), ((), ())), precision=lax.Prec...]
    all_gather x2 -> x0, blocking collectives: 77.2 us -> none  [body(): batch = lax.all_gather(picked, CEN, axis=0, tiled=True)]
    all_to_all x5 -> x0, waiting for transfers between devices: 46.9 us -> none  [the longest x3 35.3 us: sent_to_all(): lax.all_to_all(jnp.broadcast_to(x[None], (size, *x.shape)), axis, 0, 0, t...]
    all_gather x1 -> x0, waiting for transfers between devices: 42.1 us -> none  [body(): full_centres = lax.all_gather(centres, OUT, axis=1, tiled=True)]
    psum x5 -> x0, blocking collectives: 40.4 us -> none  [over_axes(): x = lax.psum(x, axis)]
    all_to_all x5 -> x0, starting transfers between devices: 29.4 us -> none  [the longest x3 15.8 us: sent_to_all(): lax.all_to_all(jnp.broadcast_to(x[None], (size, *x.shape)), axis, 0, 0, t...]
    all_to_all x1 -> x0, blocking collectives: 17.1 us -> none  [sent_to_all(): lax.all_to_all(jnp.broadcast_to(x[None], (size, *x.shape)), axis, 0, 0, t...]
  transfers between devices with their start and end apart: 6 -> 0, of which waited for: 5 -> 0; matrix products, arithmetic and copies ran while one was open for 14% -> 0% of each run, Pallas kernels for 0% -> 0%
where the time goes in v1:
time: 132 us
  Pallas kernels  128 us (97%)
  other arithmetic  2.31 us (2%)
    pallas_call x1, Pallas kernels, body(): pl.pallas_call(functools.partial(kernel, float(entries)), out_shape=(jax....  128 us

profile of v1, /device:TPU:1, one launch (start us, length us, event | category | flops | bytes accessed | tf_op | source)
XLA Modules:
  0.0 131.9 jit_solution(7088587096249886739)
XLA Ops:
  0.6 0.0 copy-start
  0.6 128.3 %step.1 = (f32[2048,128]{1,0:T(8,128)}, f32[2,16,128]{2,1,0:T(8,128)}) custom-call(s32[2,16]{1,0:T(2,128)} %idx_ref.1, f32[2048,128]{1,0:T(8,128)} %feat_ref.1, f32[2048,128]{1,0:T(8,128)} %cen_ref.1, f32[2048,125]{1,0:T(8,128)} %coef_ref.1, f32[2,16,125]{2,1,0:T(8,128)} %targ_ref.1), custom_call_target="tpu_custom_call" | custom-call | tf_op jit(solution)/shard_map/step/pallas_call | solution.py:397
  129.0 0.0 copy-done
  129.0 0.0 copy-start.1
  129.0 2.3 %slice_subtract_fusion = f32[2048,125]{1,0:T(8,128)} fusion(f32[2048,125]{1,0:T(8,128)S(1)} %copy-done, f32[2048,128]{1,0:T(8,128)} %get-tuple-element.5), kind=kLoop, calls=%fused_computation | loop fusion | flops 256000 | bytes 3072000 | tf_op jit(solution)/shard_map/sub | solution.py:412
  131.3 0.0 copy-done.1
  131.3 0.6 copy.8
Async XLA Ops:
  0.6 128.3 %copy-start = (f32[2048,125]{1,0:T(8,128)S(1)}, f32[2048,125]{1,0:T(8,128)}, u32[]{:S(2)}) copy-start(f32[2048,125]{1,0:T(8,128)} %coef_ref.1) | copy-start | bytes 3072004
  129.0 2.3 %copy-start.1 = (f32[2,16,128]{2,1,0:T(8,128)S(1)}, f32[2,16,128]{2,1,0:T(8,128)}, u32[]{:S(2)}) copy-start(f32[2,16,128]{2,1,0:T(8,128)} %get-tuple-element.4) | copy-start | bytes 49156

commit v2 on v1

v2 whole, which is shorter than its diff:
```python
import functools
import math

import jax
import jax.numpy as jnp
from jax import lax
from jax.experimental import pallas as pl
from jax.experimental.pallas import tpu as pltpu
from jax.sharding import Mesh
from jax.sharding import PartitionSpec as P

W = 1024
LANES = 128
CEN = ("cen_0", "cen_1", "cen_2")
OUT = ("out_0", "out_1")
MESH = pl.DeviceIdType.MESH
NX, NY, NZ = 4, 4, 8
F32, BF16 = jnp.float32, jnp.bfloat16


def halves(v):
    hi = v.astype(BF16)
    return hi, (v - hi.astype(F32)).astype(BF16)


def dot_rows(a, b):
    return lax.dot_general(a, b, (((1,), (1,)), ((), ())), preferred_element_type=F32)


def dot_plain(a, b):
    return lax.dot_general(a, b, (((1,), (0,)), ((), ())), preferred_element_type=F32)


EARLY = 224


def kernel(
    entries, idx_ref, feat_hbm, cen_hbm, coef_hbm, targ_hbm, new_hbm, res_ref,
    feat_ref, cen_ref, coef_ref, targ_ref,
    cpad, bs, cs, gs, cth, ctl, ghi, glo, sbh, sbl, bsq, kf, kth, ktl,
    po, psend, precv, q, rx0, s0, ry0, ry1, t1, rx1, tz, rz, rb, rhi, rlo,
    g, us, upd, e0, e1, pp,
    in_s, pl_s, pl_r, cx_s, cx_r, cy_s, cy_r, gx_s, gx_r, z_s, z_r, d_s, d_r,
    pr_s, pr_r, x0_s, x0_r, y0_s, y0_r, y1_s, y1_r, x1_s, x1_r, rz_s, rz_r,
    az_s, az_r, ay0_s, ay0_r, ax0_s, ax0_r, ax1_s, ax1_r, ay1_s, ay1_r, ad_s, ad_r,
    p_s, p_r, u_s, u_r, e_s, e_r, out_s,
):
    x, yh = lax.axis_index("out_0"), lax.axis_index("out_1")
    yl, z, c = lax.axis_index("cen_0"), lax.axis_index("cen_1"), lax.axis_index("cen_2")
    y = yh * 2 + yl
    rows = cen_ref.shape[0] // NX
    blk = yh * NX + x
    wide = coef_ref.shape[1]

    def at_x(d):
        return lax.rem(x + d, NX)

    def at_z(d):
        return lax.rem(z + d + NZ, NZ)

    def slot(i):
        return pl.ds(pl.multiple_of(i * rows, 8), rows)

    def lanes(i):
        return pl.ds(i * LANES, LANES)

    def to(dx=0, dy=0, dz=0, flip=False):
        ny = lax.rem(y + dy, NY)
        return {
            "out_0": at_x(dx), "out_1": lax.div(ny, 2), "cen_0": lax.rem(ny, 2),
            "cen_1": at_z(dz), "cen_2": 1 - c if flip else c,
        }

    pair_y = {"out_0": x, "out_1": yh, "cen_0": 1 - yl, "cen_1": z, "cen_2": c}
    plane = [(dx, dy) for dx in range(NX) for dy in range(NY) if dx or dy]
    peers = [to(dx, dy) for dx, dy in plane] + [to(dz=d) for d in range(1, NZ)] + [to(flip=True)]

    loads = [
        pltpu.make_async_copy(src, dst, in_s.at[n])
        for n, (src, dst) in enumerate(
            ((feat_hbm, feat_ref), (cen_hbm, cen_ref), (coef_hbm, coef_ref), (targ_hbm, targ_ref))
        )
    ]
    for load in loads:
        load.start()
    barrier = pltpu.get_barrier_semaphore()
    for peer in peers:
        pl.semaphore_signal(barrier, inc=1, device_id=peer, device_id_type=MESH)

    sent = []

    def send(src, dst, ss, rs, dev):
        copy = pltpu.make_async_remote_copy(
            src_ref=src, dst_ref=dst, send_sem=ss, recv_sem=rs, device_id=dev, device_id_type=MESH
        )
        copy.start()
        sent.append(copy)
        return copy

    mine = bs.at[z, c, yl, blk]
    loads[0].wait()
    for k in range(2):
        for j in range(16):
            mine[pl.ds(k * 16 + j, 1), :] = feat_ref[pl.ds(idx_ref[k, j], 1), :]
    loads[1].wait()
    cs[blk] = cen_ref[slot(x), :]
    pl.semaphore_wait(barrier, len(peers))

    got_plane = [
        send(mine, mine, pl_s.at[n], pl_r.at[n], to(dx, dy)) for n, (dx, dy) in enumerate(plane)
    ]
    got_cx = {}
    for d in (2, 1, 3):
        got_cx[d] = send(
            cen_ref.at[slot(at_x(d))], cs.at[blk], cx_s.at[d - 1], cx_r.at[d - 1], to(dx=d)
        )
    got_cy = {0: send(cen_ref.at[slot(x)], cs.at[blk], cy_s.at[0], cy_r.at[0], to(dy=2))}

    loads[2].wait()
    loads[3].wait()

    @pl.loop(0, cpad.shape[0] // 256)
    def _(i):
        at = pl.ds(pl.multiple_of(i * 256, 256), 256)
        cpad[at, :] = jnp.zeros((256, LANES), F32)
        cpad[at, pl.ds(0, wide)] = coef_ref[at, :]

    gs[x] = cpad[slot(x), :]

    for copy in got_plane:
        copy.wait_recv()
    got_z, got_d = {}, {}
    for h in range(2):
        part = bs.at[z, c, h]
        for way, dz in ((0, 1), (1, -1)):
            got_z[way, 1, h] = send(part, part, z_s.at[way, 0, h], z_r.at[way, 0, h], to(dz=dz))
    for h in range(2):
        part = bs.at[z, c, h]
        got_d[0, h] = send(part, part, d_s.at[0, h], d_r.at[0, h], to(flip=True))

    def split_rows(zs, cc, h):
        acc = [None, None]
        for b in range(2 * NX):
            for k in range(2):
                v = bs[zs, cc, h, b, pl.ds(k * 16, 16), :]
                hi, lo = halves(v)
                at = pl.ds(pl.multiple_of((k * 4 + cc * 2 + h) * 16, 16), 16)
                sbh[zs, at, lanes(b)] = hi
                sbl[zs, at, lanes(b)] = lo
                acc[k] = v * v if acc[k] is None else acc[k] + v * v
        for k in range(2):
            at = pl.ds(pl.multiple_of((k * 4 + cc * 2 + h) * 16, 16), 16)
            total = jnp.sum(acc[k], axis=1, keepdims=True)
            bsq[zs, at, :] = jnp.broadcast_to(total, (16, LANES))

    def other(rel):
        for h in range(2):
            got_d[rel, h].wait_recv()
            split_rows(at_z(rel), 1 - c, h)

    for h in range(2):
        split_rows(z, c, h)
    for d in (1, 3, 2):
        got_cx[d].wait_recv()
        part = cs.at[yh * NX + at_x(NX - d)]
        got_cy[d] = send(part, part, cy_s.at[d], cy_r.at[d], to(dy=2))
    got_g = [
        send(cpad.at[slot(at_x(d))], gs.at[x], gx_s.at[d - 1], gx_r.at[d - 1], to(dx=d))
        for d in (2, 1, 3)
    ]

    def ring_step(s):
        for h in range(2):
            for way, dz in ((0, 1), (1, -1)):
                if s == 4 and h != way:
                    continue
                got_z[way, s, h].wait_recv()
                part = bs.at[at_z(-dz * s), c, h]
                if s < 3 or (s == 3 and h == way):
                    got_z[way, s + 1, h] = send(
                        part, part, z_s.at[way, s, h], z_r.at[way, s, h], to(dz=dz)
                    )
                rel = (-dz * s) % NZ
                got_d[rel, h] = send(part, part, d_s.at[rel, h], d_r.at[rel, h], to(flip=True))
        for h in range(2):
            for way, dz in ((0, 1), (1, -1)):
                if s < 4 or h == way:
                    split_rows(at_z(-dz * s), c, h)

    def take_centres(base):
        squares = None
        for i in range(NX):
            v = cs[base + i].T
            hi, lo = halves(v)
            at = pl.ds(pl.multiple_of((base + i) * LANES, LANES), LANES)
            cth[at, :] = hi
            ctl[at, :] = lo
            squares = v * v if squares is None else squares + v * v
        return jnp.sum(squares, axis=0, keepdims=True)

    first_sq = take_centres(yh * NX)
    ring_step(1)
    other(0)
    ring_step(2)
    other(1)
    other(7)
    ring_step(3)
    other(2)
    other(6)
    for d in (0, 1, 3, 2):
        got_cy[d].wait_recv()
    centre_sq = first_sq + take_centres((1 - yh) * NX)

    def kernel_slab(rel):
        zs = at_z(rel)
        bh, bl = sbh[zs], sbl[zs]
        square = bsq[zs]
        for n in range(rows // 256):
            cat = pl.ds(n * 256, 256)
            ch, cl = cth[:, cat], ctl[:, cat]
            inner = (dot_plain(bl, cl) + dot_plain(bl, ch)) + dot_plain(bh, cl) + dot_plain(bh, ch)
            for i in range(2):
                lo = i * LANES
                sums = square + centre_sq[:, n * 256 + lo : n * 256 + lo + LANES]
                sq = sums - 2.0 * inner[:, lo : lo + LANES]
                kern = jnp.exp(jnp.sqrt(jnp.maximum(sq, 0.0)) * (-1.0 / (0.5 * math.sqrt(W))))
                for k in range(2):
                    at = pl.ds(pl.multiple_of(zs * 64, 64), 64)
                    kf[k, at, pl.ds(n * 256 + lo, LANES)] = kern[k * 64 : k * 64 + 64]

    got_p = {}

    def predict_slab(rel):
        zs = at_z(rel)
        at = pl.ds(pl.multiple_of(zs * 64, 64), 64)
        kh, kl = halves(jnp.concatenate([kf[0, at, :], kf[1, at, :]], axis=0))
        out = dot_plain(kl, ghi[...]) + dot_plain(kh, glo[...]) + dot_plain(kh, ghi[...])
        po[...] = out.reshape(2, 2, 2, 16, NX * LANES)
        zat = pl.ds(pl.multiple_of(zs * 16, 16), 16)
        for k in range(2):
            for h in range(2):
                for i in range(NX):
                    psend[zs, k, i, h] = po[k, 1 - c, h, :, lanes(i)]
        for k in range(2):
            for h in range(2):
                for i in range(NX):
                    q[k, i, h, zat, :] = po[k, c, h, :, lanes(i)]
        got_p[rel] = send(psend.at[zs], precv.at[zs], pr_s.at[rel], pr_r.at[rel], to(flip=True))

    def join(rel):
        got_p[rel].wait_recv()
        zs = at_z(rel)
        zat = pl.ds(pl.multiple_of(zs * 16, 16), 16)
        for k in range(2):
            for h in range(2):
                for i in range(NX):
                    q[k, i, h, zat, :] = q[k, i, h, zat, :] + precv[zs, k, i, h]

    for rel in (0, 1, 7, 2, 6):
        kernel_slab(rel)
    for copy in got_g:
        copy.wait_recv()
    for i in range(NX):
        hi, lo = halves(gs[i])
        ghi[:, lanes(i)] = hi
        glo[:, lanes(i)] = lo
    for rel in (3, 5):
        other(rel)
        kernel_slab(rel)
    ready = (0, 1, 7, 2, 6, 3, 5)
    for rel in ready:
        predict_slab(rel)
    ring_step(4)
    for rel in ready[:-2]:
        join(rel)
    other(4)
    kernel_slab(4)
    predict_slab(4)
    for rel in (3, 5, 4):
        join(rel)

    got_y1 = send(q.at[1, :, 1 - yl], ry1, y1_s.at[0], y1_r.at[0], pair_y)
    got_x0 = [
        send(q.at[0, at_x(d)], rx0.at[d - 1], x0_s.at[d - 1], x0_r.at[d - 1], to(dx=d))
        for d in (2, 1, 3)
    ]
    for k in range(2):
        for m in range(4):
            for n in range(rows // 128):
                hi, lo = halves(kf[k, pl.ds(m * 128, 128), lanes(n)].T)
                kth[k, pl.ds(n * 128, 128), lanes(m)] = hi
                ktl[k, pl.ds(n * 128, 128), lanes(m)] = lo
    got_y1.wait_recv()
    for i in range(NX):
        t1[i] = q[1, i, yl] + ry1[i]
    got_x1 = [
        send(t1.at[at_x(d)], rx1.at[d - 1], x1_s.at[d - 1], x1_r.at[d - 1], to(dx=d))
        for d in (2, 1, 3)
    ]
    for copy in got_x0:
        copy.wait_recv()
    for h in range(2):
        s0[h] = (q[0, x, h] + rx0[0, h]) + (rx0[1, h] + rx0[2, h])
    got_y0 = send(s0.at[1 - yl], ry0, y0_s.at[0], y0_r.at[0], pair_y)

    def spread_z(k):
        return [
            send(tz.at[k, at_z(d)], rz.at[k, d - 1], rz_s.at[k, d - 1], rz_r.at[k, d - 1], to(dz=d))
            for d in range(1, NZ)
        ]

    for copy in got_x1:
        copy.wait_recv()
    tz[1] = ((t1[x] + rx1[0]) + (rx1[1] + rx1[2])).reshape(NZ, 16, LANES)
    got_z1 = spread_z(1)
    got_y0.wait_recv()
    tz[0] = (s0[yl] + ry0[...]).reshape(NZ, 16, LANES)
    got_z0 = spread_z(0)

    def residual(k, got):
        for copy in got:
            copy.wait_recv()
        acc = tz[k, z]
        for d in range(1, NZ):
            acc = acc + rz[k, d - 1]
        at = pl.ds(pl.multiple_of(z * 16, 16), 16)
        value = acc[:, :wide] - targ_ref[k]
        rb[k, x, c, yl, at, :] = jnp.zeros((16, LANES), F32)
        rb[k, x, c, yl, at, pl.ds(0, wide)] = value
        block = rb.at[k, x, c, yl, at]
        res_ref[k] = value
        return [
            send(block, block, az_s.at[k, d - 1], az_r.at[k, d - 1], to(dz=d)) for d in range(1, NZ)
        ]

    got_a1 = residual(1, got_z1)
    got_a0 = residual(0, got_z0)

    for copy in got_a1:
        copy.wait_recv()
    part = rb.at[1, x, c, yl]
    got_ax1 = [send(part, part, ax1_s.at[d - 1], ax1_r.at[d - 1], to(dx=d)) for d in (2, 1, 3)]
    for copy in got_a0:
        copy.wait_recv()
    part = rb.at[0, x, c, yl]
    got_ay0 = send(part, part, ay0_s.at[0], ay0_r.at[0], pair_y)
    for copy in got_ax1:
        copy.wait_recv()
    part = rb.at[1, :, c, yl]
    got_ay1 = send(part, part, ay1_s.at[0], ay1_r.at[0], pair_y)
    got_ad = {1: [], 0: []}
    got_ad[1].append(send(part, part, ad_s.at[0], ad_r.at[0], to(flip=True)))
    got_ay0.wait_recv()
    part = rb.at[0, x, c]
    got_ax0 = {
        d: send(part, part, ax0_s.at[d - 1], ax0_r.at[d - 1], to(dx=d)) for d in (2, 1, 3)
    }
    got_ad[0].append(send(part, part, ad_s.at[1], ad_r.at[1], to(flip=True)))
    for d in (1, 3, 2):
        got_ax0[d].wait_recv()
        part = rb.at[0, at_x(NX - d), c]
        got_ad[0].append(send(part, part, ad_s.at[1 + d], ad_r.at[1 + d], to(flip=True)))
    got_ay1.wait_recv()
    part = rb.at[1, :, c, 1 - yl]
    got_ad[1].append(send(part, part, ad_s.at[5], ad_r.at[5], to(flip=True)))

    def gradient(k):
        for copy in got_ad[k]:
            copy.wait_recv()
        for i in range(NX):
            for cc in range(2):
                for h in range(2):
                    hi, lo = halves(rb[k, i, cc, h])
                    for zs in range(NZ):
                        at = pl.ds(zs * 64 + (cc * 2 + h) * 16, 16)
                        rhi[at, lanes(i)] = hi[zs * 16 : zs * 16 + 16]
                        rlo[at, lanes(i)] = lo[zs * 16 : zs * 16 + 16]
        acc = jnp.zeros((8, LANES), F32)
        for n in range(rows // 128):
            at = pl.ds(n * 128, 128)
            kh, kl = kth[k, at, :], ktl[k, at, :]
            out = dot_plain(kl, rhi[...]) + dot_plain(kh, rlo[...]) + dot_plain(kh, rhi[...])
            out = out * (1.0 / (2 * NZ * 2 * 16))
            for i in range(NX):
                v = out[:, i * LANES : (i + 1) * LANES]
                g[k, i, at, :] = v
                acc = acc + jnp.sum((v * v).reshape(16, 8, LANES), axis=0)
        return jnp.sum(acc, axis=0, keepdims=True)

    parts = [gradient(0), gradient(1)]

    line = lax.broadcasted_iota(jnp.int32, (8, LANES), 0)
    acc = jnp.where(line == 0, parts[0], jnp.where(line == 1, parts[1], 0.0))
    pp[0] = acc
    got = [
        send(pp.at[0], pp.at[8 + n], p_s.at[8 + n], p_r.at[8 + n], to(dx, dy))
        for n, (dx, dy) in enumerate(plane)
    ]
    first = pl.ds(0, EARLY)
    got_e = []
    for k, dst in ((0, e0), (1, e1)):
        for d in (2, 1, 3):
            got_e.append(
                send(
                    g.at[k, at_x(d), first], dst.at[d - 1], e_s.at[k, d - 1], e_r.at[k, d - 1],
                    to(dx=d),
                )
            )
    for n, copy in enumerate(got):
        copy.wait_recv()
        acc = acc + pp[8 + n]
    pp[23] = acc
    got = [send(pp.at[23], pp.at[d], p_s.at[d], p_r.at[d], to(dz=d)) for d in range(1, NZ)]
    for d, copy in enumerate(got, 1):
        copy.wait_recv()
        acc = acc + pp[d]
    pp[24] = acc
    got = send(pp.at[24], pp.at[25], p_s.at[0], p_r.at[0], to(flip=True))
    got.wait_recv()
    acc = acc + pp[25]
    sums = jnp.sum(acc, axis=1, keepdims=True)
    factor = [0.1 / jnp.sqrt(sums[k : k + 1] / entries + 1e-6) for k in range(2)]

    late = pl.ds(EARLY, rows - EARLY)
    got = {}
    for d in (2, 1, 3):
        us[d - 1] = g[0, at_x(d), late, :] * factor[0] + g[1, at_x(d), late, :] * factor[1]
        got[d] = send(us.at[d - 1], upd.at[x], u_s.at[d - 1], u_r.at[d - 1], to(dx=d))

    stores = []

    def update(i, early, rest):
        head = pl.ds(pl.multiple_of(i * rows, 8), EARLY)
        coef_ref[head, :] = coef_ref[head, :] - early[:, :wide]
        foot = pl.ds(pl.multiple_of(i * rows + EARLY, 8), rows - EARLY)
        coef_ref[foot, :] = coef_ref[foot, :] - rest[:, :wide]
        store = pltpu.make_async_copy(
            coef_ref.at[slot(i)], new_hbm.at[slot(i)], out_s.at[len(stores)]
        )
        store.start()
        stores.append(store)

    def own(at):
        return g[0, x, at, :] * factor[0] + g[1, x, at, :] * factor[1]

    update(x, own(first), own(late))
    for copy in got_e:
        copy.wait_recv()
    for d in (1, 3, 2):
        early = e0[d - 1] * factor[0] + e1[d - 1] * factor[1]
        got[d].wait_recv()
        i = at_x(NX - d)
        update(i, early, upd[i])
    for store in stores:
        store.wait()
    for copy in sent:
        copy.wait_send()


def body(features, centres, coefs, batch_index, targets):
    total = centres.shape[0]
    rows = total // NX
    entries = total * lax.axis_size(CEN) * coefs.shape[1] * lax.axis_size(OUT)
    vm = lambda *shape: pltpu.VMEM(shape, F32)
    vb = lambda *shape: pltpu.VMEM(shape, BF16)
    dma = lambda *shape: pltpu.SemaphoreType.DMA(shape)
    two = lambda *shape: [dma(*shape), dma(*shape)]
    wide = coefs.shape[1]
    scratch = [
        vm(total, LANES), vm(total, LANES), vm(total, wide), vm(*targets.shape),
        vm(total, LANES), vm(8, 2, 2, 8, 32, LANES), vm(8, rows, LANES), vm(NX, rows, LANES),
        vb(W, rows), vb(W, rows), vb(rows, 512), vb(rows, 512),
        vb(NZ, 128, W), vb(NZ, 128, W), vm(NZ, 128, LANES),
        vm(2, 512, rows), vb(2, rows, 512), vb(2, rows, 512),
        vm(2, 2, 2, 16, 512), vm(NZ, 2, NX, 2, 16, LANES), vm(NZ, 2, NX, 2, 16, LANES),
        vm(2, NX, 2, 128, LANES),
        vm(3, 2, 128, LANES), vm(2, 128, LANES), vm(128, LANES), vm(NX, 128, LANES),
        vm(NX, 128, LANES), vm(3, 128, LANES), vm(2, NZ, 16, LANES), vm(2, 7, 16, LANES),
        vm(2, NX, 2, 2, 128, LANES), vb(512, 512), vb(512, 512),
        vm(2, NX, rows, LANES), vm(3, rows - EARLY, LANES), vm(NX, rows - EARLY, LANES),
        vm(3, EARLY, LANES), vm(3, EARLY, LANES), vm(26, 8, LANES),
        dma(4), *two(15), *two(3), *two(4), *two(3), *two(2, 4, 2), *two(8, 2),
        *two(8), *two(3), *two(1), *two(1), *two(3), *two(2, 7),
        *two(2, 7), *two(1), *two(3), *two(3), *two(1), *two(6),
        *two(23), *two(3), *two(2, 3), dma(4),
    ]
    whole = pl.BlockSpec(memory_space=pltpu.VMEM)
    there = pl.BlockSpec(memory_space=pl.ANY)
    new, resid = pl.pallas_call(
        functools.partial(kernel, float(entries)),
        out_shape=(
            jax.ShapeDtypeStruct(coefs.shape, F32),
            jax.ShapeDtypeStruct(targets.shape, F32),
        ),
        in_specs=[pl.BlockSpec(memory_space=pltpu.SMEM)] + [there] * 4,
        out_specs=(there, whole),
        scratch_shapes=scratch,
        compiler_params=pltpu.CompilerParams(
            collective_id=0, has_side_effects=True, vmem_limit_bytes=60 * 2**20
        ),
        name="step",
    )(batch_index, features, centres, coefs, targets)
    return resid, new


def solution(mesh):
    torus = Mesh(mesh.devices.reshape(2, 8, 2, 4, 2), ("cen_0", "cen_1", "cen_2", "out_0", "out_1"))
    return jax.shard_map(
        body,
        mesh=torus,
        in_specs=(P(CEN, OUT), P(CEN, OUT), P(CEN, OUT), P(None, CEN), P(None, CEN, OUT)),
        out_specs=(P(None, CEN, OUT), P(CEN, OUT)),
        check_vma=False,
    )
```

time: 132 us -> 122 us (0.924)
  Pallas kernels: 128 us -> 118 us
  local copies, waits for them, and re-layouts: 0.61 us -> 3.59 us
  other arithmetic: 2.31 us -> 0 us
    pallas_call x1, Pallas kernels: 128 us -> 118 us  [body(): pl.pallas_call(functools.partial(kernel, float(entries)), out_shape=(jax....]
    unnamed x5 -> x2, local copies, waits for them, and re-layouts: 0.61 us -> 3.59 us
    sub x1 -> x0, other arithmetic: 2.31 us -> none  [body(): return (resid[:, :, :wide], coefs - upd[:, :wide])]
where the time goes in v2:
time: 122 us
  Pallas kernels  118 us (97%)
  local copies, waits for them, and re-layouts  3.59 us (3%)
    pallas_call x1, Pallas kernels, body(): pl.pallas_call(functools.partial(kernel, float(entries)), out_shape=(jax....  118 us
    unnamed x2, local copies, waits for them, and re-layouts  3.59 us

profile of v2, /device:TPU:1, one launch (start us, length us, event | category | flops | bytes accessed | tf_op | source)
XLA Modules:
  0.0 122.1 jit_solution(11612277268152405893)
XLA Ops:
  0.6 117.9 %step.1 = (f32[2048,125]{1,0:T(8,128)}, f32[2,16,125]{2,1,0:T(8,128)}) custom-call(s32[2,16]{1,0:T(2,128)} %idx_ref.1, f32[2048,128]{1,0:T(8,128)} %feat_hbm.1, f32[2048,128]{1,0:T(8,128)} %cen_hbm.1, f32[2048,125]{1,0:T(8,128)} %coef_hbm.1, f32[2,16,125]{2,1,0:T(8,128)} %targ_hbm.1), custom_call_target="tpu_custom_call" | custom-call | tf_op jit(solution)/shard_map/step/pallas_call | solution.py:489
  118.5 1.3 %copy.9 = f32[2,16,125]{2,1,0:T(8,128)} copy(f32[2,16,125]{2,1,0:T(8,128)} %get-tuple-element.8) | data formatting | bytes 32000
  119.8 2.3 %copy.10 = f32[2048,125]{1,0:T(8,128)} copy(f32[2048,125]{1,0:T(8,128)} %get-tuple-element.9) | data formatting | bytes 2048000

commit v3 on v2

--- a/solution.py
+++ b/solution.py
@@ -32,12 +32,13 @@
 
 
 EARLY = 224
+FAR_Z = (4, 3, 5, 2, 6, 1, 7)
 
 
 def kernel(
-    entries, idx_ref, feat_hbm, cen_hbm, coef_hbm, targ_hbm, new_hbm, res_ref,
-    feat_ref, cen_ref, coef_ref, targ_ref,
-    cpad, bs, cs, gs, cth, ctl, ghi, glo, sbh, sbl, bsq, kf, kth, ktl,
+    entries, idx_hbm, feat_hbm, cen_hbm, coef_hbm, targ_hbm, new_hbm, res_hbm,
+    idx_ref, res_ref, feat_ref, cen_ref, coef_ref, targ_ref,
+    cpad, bs, cs, gs, cth, ctl, ghi, glo, sbh, sbl, bsq, begun, kf, kth, ktl,
     po, psend, precv, q, rx0, s0, ry0, ry1, t1, rx1, tz, rz, rb, rhi, rlo,
     g, us, upd, e0, e1, pp,
     in_s, pl_s, pl_r, cx_s, cx_r, cy_s, cy_r, gx_s, gx_r, z_s, z_r, d_s, d_r,
@@ -73,12 +74,16 @@
 
     pair_y = {"out_0": x, "out_1": yh, "cen_0": 1 - yl, "cen_1": z, "cen_2": c}
     plane = [(dx, dy) for dx in range(NX) for dy in range(NY) if dx or dy]
+    plane.sort(key=lambda p: -(min(p[0], NX - p[0]) + min(p[1], NY - p[1])))
     peers = [to(dx, dy) for dx, dy in plane] + [to(dz=d) for d in range(1, NZ)] + [to(flip=True)]
 
     loads = [
         pltpu.make_async_copy(src, dst, in_s.at[n])
         for n, (src, dst) in enumerate(
-            ((feat_hbm, feat_ref), (cen_hbm, cen_ref), (coef_hbm, coef_ref), (targ_hbm, targ_ref))
+            (
+                (feat_hbm, feat_ref), (cen_hbm, cen_ref), (coef_hbm, coef_ref), (targ_hbm, targ_ref),
+                (idx_hbm, idx_ref),
+            )
         )
     ]
     for load in loads:
@@ -98,6 +103,7 @@
         return copy
 
     mine = bs.at[z, c, yl, blk]
+    loads[4].wait()
     loads[0].wait()
     for k in range(2):
         for j in range(16):
@@ -160,7 +166,7 @@
 
     for h in range(2):
         split_rows(z, c, h)
-    for d in (1, 3, 2):
+    for d in (2, 1, 3):
         got_cx[d].wait_recv()
         part = cs.at[yh * NX + at_x(NX - d)]
         got_cy[d] = send(part, part, cy_s.at[d], cy_r.at[d], to(dy=2))
@@ -198,27 +204,40 @@
             squares = v * v if squares is None else squares + v * v
         return jnp.sum(squares, axis=0, keepdims=True)
 
+    def products(zs, part, cat):
+        at = pl.ds(pl.multiple_of(part * NX * LANES, LANES), NX * LANES)
+        bh, bl = sbh[zs, :, at], sbl[zs, :, at]
+        ch, cl = cth[at, cat], ctl[at, cat]
+        return (dot_plain(bl, cl) + dot_plain(bl, ch)) + dot_plain(bh, cl) + dot_plain(bh, ch)
+
+    def begin_slab(rel):
+        zs = at_z(rel)
+        for n in range(rows // 256):
+            cat = pl.ds(n * 256, 256)
+            begun[zs, :, cat] = products(zs, yh, cat)
+
     first_sq = take_centres(yh * NX)
     ring_step(1)
     other(0)
     ring_step(2)
-    other(1)
-    other(7)
+    for rel in (1, 7):
+        other(rel)
+    for rel in (0, 1, 7):
+        begin_slab(rel)
     ring_step(3)
-    other(2)
-    other(6)
+    for rel in (2, 6):
+        other(rel)
+        begin_slab(rel)
     for d in (0, 1, 3, 2):
         got_cy[d].wait_recv()
     centre_sq = first_sq + take_centres((1 - yh) * NX)
 
     def kernel_slab(rel):
         zs = at_z(rel)
-        bh, bl = sbh[zs], sbl[zs]
         square = bsq[zs]
         for n in range(rows // 256):
             cat = pl.ds(n * 256, 256)
-            ch, cl = cth[:, cat], ctl[:, cat]
-            inner = (dot_plain(bl, cl) + dot_plain(bl, ch)) + dot_plain(bh, cl) + dot_plain(bh, ch)
+            inner = begun[zs, :, cat] + products(zs, 1 - yh, cat)
             for i in range(2):
                 lo = i * LANES
                 sums = square + centre_sq[:, n * 256 + lo : n * 256 + lo + LANES]
@@ -266,6 +285,7 @@
         glo[:, lanes(i)] = lo
     for rel in (3, 5):
         other(rel)
+        begin_slab(rel)
         kernel_slab(rel)
     ready = (0, 1, 7, 2, 6, 3, 5)
     for rel in ready:
@@ -274,6 +294,7 @@
     for rel in ready[:-2]:
         join(rel)
     other(4)
+    begin_slab(4)
     kernel_slab(4)
     predict_slab(4)
     for rel in (3, 5, 4):
@@ -306,7 +327,7 @@
     def spread_z(k):
         return [
             send(tz.at[k, at_z(d)], rz.at[k, d - 1], rz_s.at[k, d - 1], rz_r.at[k, d - 1], to(dz=d))
-            for d in range(1, NZ)
+            for d in FAR_Z
         ]
 
     for copy in got_x1:
@@ -330,11 +351,13 @@
         block = rb.at[k, x, c, yl, at]
         res_ref[k] = value
         return [
-            send(block, block, az_s.at[k, d - 1], az_r.at[k, d - 1], to(dz=d)) for d in range(1, NZ)
+            send(block, block, az_s.at[k, d - 1], az_r.at[k, d - 1], to(dz=d)) for d in FAR_Z
         ]
 
     got_a1 = residual(1, got_z1)
     got_a0 = residual(0, got_z0)
+    keep = pltpu.make_async_copy(res_ref, res_hbm, in_s.at[5])
+    keep.start()
 
     for copy in got_a1:
         copy.wait_recv()
@@ -410,8 +433,8 @@
         copy.wait_recv()
         acc = acc + pp[8 + n]
     pp[23] = acc
-    got = [send(pp.at[23], pp.at[d], p_s.at[d], p_r.at[d], to(dz=d)) for d in range(1, NZ)]
-    for d, copy in enumerate(got, 1):
+    got = [send(pp.at[23], pp.at[d], p_s.at[d], p_r.at[d], to(dz=d)) for d in FAR_Z]
+    for d, copy in zip(FAR_Z, got):
         copy.wait_recv()
         acc = acc + pp[d]
     pp[24] = acc
@@ -453,6 +476,7 @@
         update(i, early, upd[i])
     for store in stores:
         store.wait()
+    keep.wait()
     for copy in sent:
         copy.wait_send()
 
@@ -467,11 +491,12 @@
     two = lambda *shape: [dma(*shape), dma(*shape)]
     wide = coefs.shape[1]
     scratch = [
+        pltpu.SMEM(batch_index.shape, jnp.int32), vm(*targets.shape),
         vm(total, LANES), vm(total, LANES), vm(total, wide), vm(*targets.shape),
         vm(total, LANES), vm(8, 2, 2, 8, 32, LANES), vm(8, rows, LANES), vm(NX, rows, LANES),
         vb(W, rows), vb(W, rows), vb(rows, 512), vb(rows, 512),
         vb(NZ, 128, W), vb(NZ, 128, W), vm(NZ, 128, LANES),
-        vm(2, 512, rows), vb(2, rows, 512), vb(2, rows, 512),
+        vm(NZ, 128, rows), vm(2, 512, rows), vb(2, rows, 512), vb(2, rows, 512),
         vm(2, 2, 2, 16, 512), vm(NZ, 2, NX, 2, 16, LANES), vm(NZ, 2, NX, 2, 16, LANES),
         vm(2, NX, 2, 128, LANES),
         vm(3, 2, 128, LANES), vm(2, 128, LANES), vm(128, LANES), vm(NX, 128, LANES),
@@ -479,12 +504,11 @@
         vm(2, NX, 2, 2, 128, LANES), vb(512, 512), vb(512, 512),
         vm(2, NX, rows, LANES), vm(3, rows - EARLY, LANES), vm(NX, rows - EARLY, LANES),
         vm(3, EARLY, LANES), vm(3, EARLY, LANES), vm(26, 8, LANES),
-        dma(4), *two(15), *two(3), *two(4), *two(3), *two(2, 4, 2), *two(8, 2),
+        dma(6), *two(15), *two(3), *two(4), *two(3), *two(2, 4, 2), *two(8, 2),
         *two(8), *two(3), *two(1), *two(1), *two(3), *two(2, 7),
         *two(2, 7), *two(1), *two(3), *two(3), *two(1), *two(6),
         *two(23), *two(3), *two(2, 3), dma(4),
     ]
-    whole = pl.BlockSpec(memory_space=pltpu.VMEM)
     there = pl.BlockSpec(memory_space=pl.ANY)
     new, resid = pl.pallas_call(
         functools.partial(kernel, float(entries)),
@@ -492,8 +516,8 @@
             jax.ShapeDtypeStruct(coefs.shape, F32),
             jax.ShapeDtypeStruct(targets.shape, F32),
         ),
-        in_specs=[pl.BlockSpec(memory_space=pltpu.SMEM)] + [there] * 4,
-        out_specs=(there, whole),
+        in_specs=[there] * 5,
+        out_specs=(there, there),
         scratch_shapes=scratch,
         compiler_params=pltpu.CompilerParams(
             collective_id=0, has_side_effects=True, vmem_limit_bytes=60 * 2**20

time: 122 us -> 116 us (0.951)
  Pallas kernels: 118 us -> 112 us
    pallas_call x1, Pallas kernels: 118 us -> 112 us  [body(): pl.pallas_call(functools.partial(kernel, float(entries)), out_shape=(jax....]
where the time goes in v3:
time: 116 us
  Pallas kernels  112 us (97%)
  local copies, waits for them, and re-layouts  3.59 us (3%)
    pallas_call x1, Pallas kernels, body(): pl.pallas_call(functools.partial(kernel, float(entries)), out_shape=(jax....  112 us
    unnamed x2, local copies, waits for them, and re-layouts  3.59 us

profile of v3, /device:TPU:1, one launch (start us, length us, event | category | flops | bytes accessed | tf_op | source)
XLA Modules:
  0.0 116.3 jit_solution(2277169122995596937)
XLA Ops:
  0.6 112.0 %step.1 = (f32[2048,125]{1,0:T(8,128)}, f32[2,16,125]{2,1,0:T(8,128)}) custom-call(s32[2,16]{1,0:T(2,128)} %idx_hbm.1, f32[2048,128]{1,0:T(8,128)} %feat_hbm.1, f32[2048,128]{1,0:T(8,128)} %cen_hbm.1, f32[2048,125]{1,0:T(8,128)} %coef_hbm.1, f32[2,16,125]{2,1,0:T(8,128)} %targ_hbm.1), custom_call_target="tpu_custom_call" | custom-call | tf_op jit(solution)/shard_map/step/pallas_call | solution.py:513
  112.7 1.3 %copy.9 = f32[2,16,125]{2,1,0:T(8,128)} copy(f32[2,16,125]{2,1,0:T(8,128)} %get-tuple-element.8) | data formatting | bytes 32000
  114.0 2.3 %copy.10 = f32[2048,125]{1,0:T(8,128)} copy(f32[2048,125]{1,0:T(8,128)} %get-tuple-element.9) | data formatting | bytes 2048000
